TPU v7x, 512 devices: a whole 4x4x16 slice. The times are simulated.
512 devices in a mesh: cuts: 16 (over y, x_hi, core), grid: 32 (over z, x_lo).
Axes of the slice: x: 4 (x_hi: 2, x_lo: 2; x = x_hi * 2 + x_lo), y: 4, z: 16, core: 2. Of those that a mesh axis runs over, the one named last changes fastest.
Arguments:
- orbitals: bfloat16 [131072, 4096], P('grid', 'cuts'), may hold values from -9 to 9, as said below
- potential: float32 [131072], P('grid'), may hold values from -1 to 1
- core_density: float32 [131072], P('grid'), may hold values from 0.05 to 0.5
- occupation: int32 [4096], P('cuts'), may hold values from 0 to 2
- slice_counts: int32 [16], P('cuts'), may hold values from 128 to 256
Outputs:
- orbitals_out: bfloat16 [131072, 4096], P('grid', 'cuts')
- potential_out: float32 [131072], P('grid')
Inputs may be any that keep to these rules, and one draw needn't show every extreme that they name: `orbitals`: every entry has magnitude at most 9.
All inputs are finite; a program needn't handle non-finite values.
Results may differ from a plain program's by a relative error of at most 0.0015.
The roundings to bfloat16 on the way count: a program that leaves them out, or rounds other values in their place, can miss the bound.
Values may be sent and summed in bfloat16 or wider, within the bound.
No kernel may reach another device: no remote copies, remote signals or barrier semaphores. Data moves between devices by JAX's collectives and lax.ppermute only.
A program may use at most 64 MiB of HBM per device.

v0:
```python
import jax
import jax.numpy as jnp
from jax import lax
from jax.sharding import Mesh
from jax.sharding import PartitionSpec as P

GRID = ("grid_0", "grid_1")


mixing = 0.3
step_size = 0.5


def with_halo(x, sides, width):
    for axis, dim in sides:
        peers, length = (lax.axis_size(axis), x.shape[dim])
        up = [(i, (i + 1) % peers) for i in range(peers)]
        down = [(j, i) for i, j in up]
        last = lax.slice_in_dim(x, length - width, length, axis=dim)
        leading = lax.slice_in_dim(x, 0, width, axis=dim)
        before = lax.ppermute(last, axis, up)
        after = lax.ppermute(leading, axis, down)
        x = jnp.concatenate([before, x, after], axis=dim)
    return x


def cut_along(x, dim, peers):
    before, after = (x.shape[:dim], x.shape[dim + 1 :])
    return jnp.moveaxis(x.reshape(*before, peers, -1, *after), dim, 0)


def summed_on_arrival(x, axis, dim):
    blocks = cut_along(x, dim, lax.axis_size(axis))
    arrived = lax.all_to_all(blocks, axis, split_axis=0, concat_axis=0, tiled=True)
    return arrived.sum(axis=0)


def gather_axes(x, axes, dim):
    for axis in reversed(axes):
        x = lax.all_gather(x, axis, axis=dim, tiled=True)
    return x


def copy_for_each(x, axis):
    peers = lax.axis_size(axis)
    return lax.all_to_all(jnp.broadcast_to(x[None], (peers, *x.shape)), axis, 0, 0, tiled=True)


def over_copies(x, axis):
    return copy_for_each(x, axis).sum(axis=0)


def per_device(orbitals, potential, core_density, occupation, slice_counts):
    highest = lax.Precision.HIGHEST
    coefficient = (3.0 / jnp.pi) ** (1.0 / 3.0)
    rows = orbitals.shape[0]
    width = orbitals.shape[1]
    total_points = rows * lax.axis_size(GRID)
    total_states = width * lax.axis_size("cuts")
    padded = with_halo(orbitals, ((GRID, 0),), 1).astype(jnp.float32)
    middle = padded[1:-1]
    kinetic = -0.5 * (padded[2:] + padded[:-2] - 2.0 * middle)
    applied = (kinetic + potential[:, None] * middle).astype(jnp.bfloat16)
    stacked = jnp.concatenate([orbitals, applied], axis=1)
    contract = (((0,), (0,)), ((), ()))
    owned = summed_on_arrival(
        lax.dot_general(orbitals, stacked, contract, preferred_element_type=jnp.float32), GRID, 0
    )
    summed = gather_axes(owned, GRID, 0)
    intersection = summed[:, :width] / total_points
    ritz = summed[:, width:] / total_points
    factor = jnp.linalg.cholesky(intersection)
    identity = jnp.eye(width, dtype=jnp.float32)
    inverse = lax.linalg.triangular_solve(factor, identity, left_side=True, lower=True)
    projected = jnp.dot(jnp.dot(inverse, ritz, precision=highest), inverse.T, precision=highest)
    rotation = jnp.dot(inverse.T, identity - step_size * projected, precision=highest).astype(
        jnp.bfloat16
    )
    rotated = jnp.dot(orbitals, rotation, preferred_element_type=jnp.float32)
    orbitals_out = rotated.astype(jnp.bfloat16)
    live = (jnp.arange(width) < slice_counts[0]).astype(jnp.float32)
    weights = occupation.astype(jnp.float32) * live / (2.0 * total_states)
    contribution = jnp.sum(rotated * rotated * weights[None, :], axis=1)
    density = core_density + over_copies(contribution, "cuts")
    potential_out = (1.0 - mixing) * potential + mixing * (-coefficient * jnp.cbrt(density))
    return (orbitals_out, potential_out)


def solution(mesh):
    torus = Mesh(mesh.devices.reshape(mesh.shape["cuts"], 16, 2), ("cuts", "grid_0", "grid_1"))
    in_specs = (P(GRID, "cuts"), P(GRID), P(GRID), P("cuts"), P("cuts"))
    out_specs = (P(GRID, "cuts"), P(GRID))
    return jax.shard_map(
        per_device, mesh=torus, in_specs=in_specs, out_specs=out_specs, check_vma=False
    )
```

profile of v0, /device:TPU:1, one launch (start us, length us, event | category | flops | bytes accessed | tf_op | source)
XLA Modules:
  0.0 192.9 jit_solution(6424992493287388279)
XLA Ops:
  0.6 0.7 fusion.31
  1.3 3.9 %collective-permute-start = (bf16[1,256]{1,0:T(2,128)(2,1)S(1)}, bf16[1,256]{1,0:T(2,128)(2,1)S(1)}, u32[]{:S(2)}, u32[]{:S(2)}) collective-permute-start(bf16[1,256]{1,0:T(2,128)(2,1)S(1)} %get-tuple-element.31), channel_id=1, source_target_pairs={{0,1},{1,2},{2,3},{3,4},{4,5},{5,6},{6,7},{7,8},{8,9},{9,10},{10,1... | collective-permute-start | bytes 1544 | tf_op jit(solution)/shard_map/ppermute | solution.py:21
  5.3 10.9 %collective-permute-start.1 = (bf16[1,256]{1,0:T(2,128)(2,1)S(1)}, bf16[1,256]{1,0:T(2,128)(2,1)S(1)}, u32[]{:S(2)}, u32[]{:S(2)}) collective-permute-start(bf16[1,256]{1,0:T(2,128)(2,1)S(1)} %get-tuple-element.30), channel_id=1, source_target_pairs={{1,0},{2,1},{3,2},{4,3},{5,4},{6,5},{7,6},{8,7},{9,8},{10,9},{11,1... | collective-permute-start | bytes 1544 | tf_op jit(solution)/shard_map/ppermute | solution.py:22
  16.1 0.7 collective-permute-done.1
  16.8 9.2 %concatenate.8 = bf16[4098,256]{1,0:T(8,128)(2,1)S(1)} concatenate(bf16[1,256]{1,0:T(2,128)(2,1)S(1)} %collective-permute-done, bf16[4096,256]{1,0:T(8,128)(2,1)} %param.5, bf16[1,256]{1,0:T(2,128)(2,1)S(1)} %collective-permute-done.1), dimensions={0} | concatenate | bytes 4196352 | tf_op jit(solution)/shard_map/concatenate | solution.py:23
  26.8 1.5 fusion.3
  28.4 2.1 %fusion.8 = f32[32,8,512]{2,1,0:T(8,128)} fusion(bf16[4096,256]{1,0:T(8,128)(2,1)S(1)} %copy-done, bf16[4096,256]{1,0:T(8,128)(2,1)S(1)} %fusion.3), kind=kOutput, calls=%fused_computation.13 | convolution fusion | flops 1082130432 | bytes 4718592 | tf_op jit(solution)/shard_map/dot_general | solution.py:67
  30.5 10.0 %all-to-all-start = ((f32[32,8,512]{2,1,0:T(8,128)}), f32[32,8,512]{2,1,0:T(8,128)S(1)}, u32[]{:S(2)}, u32[]{:S(2)}) async-start(f32[32,8,512]{2,1,0:T(8,128)} %fusion.8), calls=%async_computation | async-start | bytes 1048576 | tf_op jit(solution)/shard_map/all_to_all | solution.py:34
  41.3 29.3 %all-to-all-done = f32[32,8,512]{2,1,0:T(8,128)S(1)} async-done(((f32[32,8,512]{2,1,0:T(8,128)}), f32[32,8,512]{2,1,0:T(8,128)S(1)}, u32[]{:S(2)}, u32[]{:S(2)}) %all-to-all-start) | async-done | bytes 524320 | tf_op jit(solution)/shard_map/all_to_all | solution.py:34
  70.6 3.5 %all_gather.6 = f32[16,512]{1,0:T(8,128)S(1)} all-gather(f32[8,512]{1,0:T(8,128)S(1)} %reduce_sum.27), channel_id=1, replica_groups=mesh['cuts'=16,'grid_0'=16,'grid_1'=2] {'grid_1'}, dimensions={0}, use_global_device_ids=true | all-gather | bytes 49152 | tf_op jit(solution)/shard_map/all_gather | solution.py:40
  74.1 22.9 %all_gather.7 = f32[256,512]{1,0:T(8,128)S(1)} all-gather(f32[16,512]{1,0:T(8,128)S(1)} %all_gather.6), channel_id=1, replica_groups=mesh['cuts'=16,'grid_0'=16,'grid_1'=2] {'grid_0'}, dimensions={0}, use_global_device_ids=true | all-gather | bytes 557056 | tf_op jit(solution)/shard_map/all_gather | solution.py:40
  97.4 11.7 %cholesky.50 = f32[128,128]{1,0:T(8,128)S(1)} custom-call(f32[128,128]{1,0:T(8,128)S(1)} %cholesky.118), custom_call_target="Cholesky" | custom-call | tf_op jit(solution)/shard_map/jit(cholesky)/cholesky | solution.py:72
  109.2 9.8 %custom-call.14 = f32[1,128,128]{1,2,0:T(8,128)S(1)} custom-call(f32[1,128,128]{2,1,0:T(8,128)S(1)} %get-tuple-element.37), custom_call_target="InvertDiagBlocksLowerTriangular" | custom-call | tf_op jit(solution)/shard_map/jit(cholesky)/cholesky | solution.py:72
  119.5 11.7 %cholesky.105 = f32[128,128]{1,0:T(8,128)S(1)} custom-call(f32[128,128]{1,0:T(8,128)S(1)} %convolution_subtract_fusion.1), custom_call_target="Cholesky" | custom-call | tf_op jit(solution)/shard_map/jit(cholesky)/cholesky | solution.py:72
  131.3 0.6 compare_reduce_fusion
  133.3 5.4 %while.1 = (s32[]{:T(128)}, f32[256,256]{1,0:T(8,128)S(1)}, s32[2,2]{1,0:T(2,128)S(1)}, f32[2,128,128]{2,1,0:T(8,128)}, s32[]{:T(128)}) while((s32[]{:T(128)}, f32[256,256]{1,0:T(8,128)S(1)}, s32[2,2]{1,0:T(2,128)S(1)}, f32[2,128,128]{2,1,0:T(8,128)}, s32[]{:T(128)}) %tuple.34), condition=%wide.while_cond, body=%wide.while_body.sunk | while | flops 2 | bytes 132705 | solution.py:74
  134.1 2.0 %bitcast_dynamic-update-slice_fusion.2 = f32[2,128,128]{2,1,0:T(8,128)} fusion(f32[2,128,128]{2,1,0:T(8,128)} %get-tuple-element.79, s32[]{:T(128)} %get-tuple-element.76, f32[256,256]{1,0:T(8,128)S(1)} %get-tuple-element.82, s32[]{:T(128)} %bitcast.41, s32[]{:T(128)} %bitcast.42), kind=kLoop, calls=%fused_computation.clone.1 | loop fusion | bytes 132608 | tf_op jit(solution)/shard_map/triangular_solve
  136.7 2.0 %bitcast_dynamic-update-slice_fusion.2 = f32[2,128,128]{2,1,0:T(8,128)} fusion(f32[2,128,128]{2,1,0:T(8,128)} %get-tuple-element.79, s32[]{:T(128)} %get-tuple-element.76, f32[256,256]{1,0:T(8,128)S(1)} %get-tuple-element.82, s32[]{:T(128)} %bitcast.41, s32[]{:T(128)} %bitcast.42), kind=kLoop, calls=%fused_computation.clone.1 | loop fusion | bytes 132608 | tf_op jit(solution)/shard_map/triangular_solve
  138.7 20.5 %custom-call.15 = f32[2,128,128]{1,2,0:T(8,128)S(1)} custom-call(f32[2,128,128]{2,1,0:T(8,128)} %get-tuple-element.9), custom_call_target="InvertDiagBlocksLowerTriangular" | custom-call | tf_op jit(solution)/shard_map/triangular_solve | solution.py:74
  161.6 2.6 %multiply_reduce_fusion = (f32[4096]{0:T(1024)S(1)}, bf16[4096,256]{0,1:T(8,128)(2,1)}) fusion(f32[256]{0:T(256)S(1)} %fusion.24, bf16[256,256]{1,0:T(8,128)(2,1)S(1)} %convolution_convert_fusion, bf16[4096,256]{1,0:T(8,128)(2,1)S(1)} %copy-done), kind=kOutput, calls=%fused_computation.11 | convolution fusion | flops 541061120 | bytes 4342784 | tf_op jit(solution)/shard_map/dot_general | solution.py:79
  164.2 0.9 broadcast_in_dim.4
  165.1 18.3 %all-to-all-start.1 = ((f32[16,1,4096]{2,1,0:T(1,128)}), f32[16,1,4096]{2,1,0:T(1,128)S(1)}, u32[]{:S(2)}, u32[]{:S(2)}) async-start(f32[16,1,4096]{2,1,0:T(1,128)} %broadcast_in_dim.4), calls=%async_computation.1 | async-start | bytes 524288 | tf_op jit(solution)/shard_map/all_to_all | solution.py:46
  183.4 4.1 %copy.21 = bf16[4096,256]{1,0:T(8,128)(2,1)} copy(bf16[4096,256]{0,1:T(8,128)(2,1)} %get-tuple-element.29) | data formatting | bytes 4194304
  187.5 4.6 %all-to-all-done.1 = f32[16,1,4096]{2,1,0:T(1,128)S(1)} async-done(((f32[16,1,4096]{2,1,0:T(1,128)}), f32[16,1,4096]{2,1,0:T(1,128)S(1)}, u32[]{:S(2)}, u32[]{:S(2)}) %all-to-all-start.1) | async-done | bytes 262176 | tf_op jit(solution)/shard_map/all_to_all | solution.py:46
  (42 shorter events, 6.3 us)
Async XLA Ops:
  1.3 14.8 %collective-permute-start = (bf16[1,256]{1,0:T(2,128)(2,1)S(1)}, bf16[1,256]{1,0:T(2,128)(2,1)S(1)}, u32[]{:S(2)}, u32[]{:S(2)}) collective-permute-start(bf16[1,256]{1,0:T(2,128)(2,1)S(1)} %get-tuple-element.31), channel_id=1, source_target_pairs={{0,1},{1,2},{2,3},{3,4},{4,5},{5,6},{6,7},{7,8},{8,9},{9,10},{10,1... | collective-permute-start | bytes 1544 | tf_op jit(solution)/shard_map/ppermute | solution.py:21
  5.3 11.6 %collective-permute-start.1 = (bf16[1,256]{1,0:T(2,128)(2,1)S(1)}, bf16[1,256]{1,0:T(2,128)(2,1)S(1)}, u32[]{:S(2)}, u32[]{:S(2)}) collective-permute-start(bf16[1,256]{1,0:T(2,128)(2,1)S(1)} %get-tuple-element.30), channel_id=1, source_target_pairs={{1,0},{2,1},{3,2},{4,3},{5,4},{6,5},{7,6},{8,7},{9,8},{10,9},{11,1... | collective-permute-start | bytes 1544 | tf_op jit(solution)/shard_map/ppermute | solution.py:22
  26.1 0.7 copy-start.1
  26.8 1.6 copy-start
  28.4 12.9 %copy-start.3 = (s32[256]{0:T(256)S(1)}, s32[256]{0:T(256)}, u32[]{:S(2)}) copy-start(s32[256]{0:T(256)} %param.8) | copy-start | bytes 3076
  30.5 40.1 %all-to-all-start = ((f32[32,8,512]{2,1,0:T(8,128)}), f32[32,8,512]{2,1,0:T(8,128)S(1)}, u32[]{:S(2)}, u32[]{:S(2)}) async-start(f32[32,8,512]{2,1,0:T(8,128)} %fusion.8), calls=%async_computation | async-start | bytes 1048576 | tf_op jit(solution)/shard_map/all_to_all | solution.py:34
  161.6 30.7 %copy-start.2 = (f32[4096]{0:T(1024)S(1)}, f32[4096]{0:T(1024)}, u32[]{:S(2)}) copy-start(f32[4096]{0:T(1024)} %param.7) | copy-start | bytes 49156
  165.1 27.0 %all-to-all-start.1 = ((f32[16,1,4096]{2,1,0:T(1,128)}), f32[16,1,4096]{2,1,0:T(1,128)S(1)}, u32[]{:S(2)}, u32[]{:S(2)}) async-start(f32[16,1,4096]{2,1,0:T(1,128)} %broadcast_in_dim.4), calls=%async_computation.1 | async-start | bytes 524288 | tf_op jit(solution)/shard_map/all_to_all | solution.py:46
where the time goes:
time: 194 us; the launch traced here: 193 us
  other arithmetic  57.3 us (30%)
  starting transfers between devices  43.1 us (22%)
  waiting for transfers between devices  34.6 us (18%)
  blocking collectives  26.4 us (14%)
  local copies, waits for them, and re-layouts  21.1 us (11%)
  matrix products  7.43 us (4%)
  between operations  2.84 us (1%)
    another operation x6, other arithmetic, per_device(): factor = jnp.linalg.cholesky(intersection)  33.9 us
    all_to_all x1, waiting for transfers between devices, summed_on_arrival(): lax.all_to_all(blocks, axis, split_axis=0, concat_axis=0, tiled=True)  29.3 us
    all_gather x2, blocking collectives, gather_axes(): x = lax.all_gather(x, axis, axis=dim, tiled=True)  26.4 us
    another operation x3, other arithmetic, per_device(): lax.linalg.triangular_solve(factor, identity, left_side=True, lower=True)  20.5 us
    all_to_all x1, starting transfers between devices, copy_for_each(): lax.all_to_all(jnp.broadcast_to(x[None], (peers, *x.shape)), axis, 0, 0,...  18.3 us
    ppermute x1, starting transfers between devices, with_halo(): after = lax.ppermute(leading, axis, down)  10.9 us
    all_to_all x1, starting transfers between devices, summed_on_arrival(): lax.all_to_all(blocks, axis, split_axis=0, concat_axis=0, tiled=True)  10 us
    concatenate x1, local copies, waits for them, and re-layouts, with_halo(): x = jnp.concatenate([before, x, after], axis=dim)  9.22 us
  transfers between devices with their start and end apart: 4, of which 3 were waited for; matrix products, arithmetic and copies ran while one was open for 2% of the time, Pallas kernels for 0%

commit v1 on v0

v1 whole, which is shorter than its diff:
```python
import jax
import jax.numpy as jnp
from jax import lax
from jax.experimental import pallas as pl
from jax.experimental.pallas import tpu as pltpu
from jax.sharding import Mesh
from jax.sharding import PartitionSpec as P

GRID = ("grid_0", "grid_1")
HIGHEST = lax.Precision.HIGHEST
F32 = jnp.float32
BF16 = jnp.bfloat16

mixing = 0.3
step_size = 0.5

PANEL = 64
CHUNK = 512
EDGE = 16


def row_dot(a, b, precision=None):
    return lax.dot_general(a, b, (((0,), (0,)), ((), ())), precision=precision, preferred_element_type=F32)


def gram_kernel(psi_ref, potential_ref, out_ref, psi_v, applied_v, sems):
    rows, width = psi_ref.shape
    n = rows // CHUNK
    copies = [
        pltpu.make_async_copy(
            psi_ref.at[pl.ds(c * CHUNK, CHUNK)], psi_v.at[pl.ds(EDGE + c * CHUNK, CHUNK)], sems.at[c]
        )
        for c in range(n)
    ]
    for copy in copies:
        copy.start()
    psi_v[0:EDGE] = jnp.zeros((EDGE, width), BF16)
    psi_v[EDGE + rows : EDGE + rows + EDGE] = jnp.zeros((EDGE, width), BF16)
    by_row = jnp.transpose(potential_ref[...])
    copies[0].wait()
    intersection = ritz = None
    for c in range(n):
        if c + 1 < n:
            copies[c + 1].wait()
        for s in range(CHUNK // 128):
            start = c * CHUNK + s * 128
            block = start // 128
            wide = psi_v[start : start + 128 + 2 * EDGE].astype(F32)
            length = wide.shape[0]
            after = pltpu.roll(wide, length - 1, 0)[EDGE : EDGE + 128]
            before = pltpu.roll(wide, 1, 0)[EDGE : EDGE + 128]
            middle = wide[EDGE : EDGE + 128]
            kinetic = -0.5 * (after + before - 2.0 * middle)
            applied_v[start : start + 128] = (kinetic + by_row[:, block : block + 1] * middle).astype(BF16)
        psi = psi_v[EDGE + c * CHUNK : EDGE + (c + 1) * CHUNK]
        applied = applied_v[c * CHUNK : (c + 1) * CHUNK]
        one, two = row_dot(psi, psi), row_dot(psi, applied)
        intersection = one if c == 0 else intersection + one
        ritz = two if c == 0 else ritz + two
    out_ref[:, :width] = intersection
    out_ref[:, width:] = ritz


def pack_kernel(gram_ref, last_ref, next_ref, out_ref):
    width = gram_ref.shape[0]
    zeros = jnp.zeros((14, width), F32)
    last, following = last_ref[...].astype(F32), next_ref[...].astype(F32)
    left = jnp.concatenate([last, following, zeros], axis=0).astype(BF16)
    right = jnp.concatenate([following, last, zeros], axis=0).astype(BF16)
    across = row_dot(left, right)
    for i in range(width // 8):
        diagonal = jnp.zeros((1, 128), F32)
        for h in range(width // 128):
            intersection = gram_ref[8 * i : 8 * i + 8, 128 * h : 128 * h + 128]
            ritz = gram_ref[8 * i : 8 * i + 8, width + 128 * h : width + 128 * h + 128]
            ritz = ritz - 0.5 * across[8 * i : 8 * i + 8, 128 * h : 128 * h + 128]
            row = lax.broadcasted_iota(jnp.int32, (8, 128), 0) + 8 * i
            col = lax.broadcasted_iota(jnp.int32, (8, 128), 1) + 128 * h
            out_ref[17 * i + 8 * h : 17 * i + 8 * h + 8] = jnp.where(row >= col, intersection, ritz)
            if 8 * i // 128 == h:
                diagonal = jnp.sum(jnp.where(row == col, ritz, 0.0), axis=0, keepdims=True)
        out_ref[17 * i + 16 : 17 * i + 17] = diagonal


def eliminate(rows, base):
    n = len(rows)
    row = lax.broadcasted_iota(jnp.int32, (8, 128), 0)
    lane = lax.broadcasted_iota(jnp.int32, (8, 128), 1)
    pivots = []
    for p in range(n):
        c = base + 8 * p
        h, l = c // 128, c % 128
        cols = [[jnp.broadcast_to(rows[t][h][:, l + j : l + j + 1], (8, 128)) for j in range(8)] for t in range(p, n)]
        inside = (lane >= l) & (lane < l + 8)
        rows[p][h] = jnp.where(inside, jnp.where(lane - l == row, 1.0, 0.0), rows[p][h])
        for t in range(p + 1, n):
            rows[t][h] = jnp.where(inside, 0.0, rows[t][h])
        pivot = None
        for k in range(8):
            spread = lambda v: jnp.broadcast_to(v[k : k + 1, :], (8, 128))
            d = spread(cols[0][k])
            pivot = d if k == 0 else jnp.where(row >= k, d, pivot)
            r = 1.0 / d
            above = {j: spread(cols[0][j]) for j in range(k + 1, 8)}
            pivot_row = [spread(rows[p][s]) for s in range(2)]
            for t in range(p, n):
                if t == p and k == 7:
                    continue
                i = t - p
                f = cols[i][k] * r
                if t == p:
                    f = jnp.where(row > k, f, 0.0)
                for j in range(k + 1, 8):
                    cols[i][j] = cols[i][j] - f * above[j]
                for s in range(2):
                    rows[t][s] = rows[t][s] - f * pivot_row[s]
        pivots.append(pivot)
    return rows, pivots


def factor(a_ref, w_ref, g_ref):
    row = lax.broadcasted_iota(jnp.int32, (8, 128), 0)
    lane = lax.broadcasted_iota(jnp.int32, (8, 128), 1)
    width = a_ref.shape[0]
    for o in range(0, width, PANEL):
        end = o + PANEL
        rows = [[a_ref[o + 8 * t : o + 8 * t + 8, 128 * h : 128 * h + 128] for h in range(2)] for t in range(PANEL // 8)]
        rows, pivots = eliminate(rows, o)
        for t in range(PANEL // 8):
            scale = lax.rsqrt(pivots[t])
            for h in range(2):
                col = lane + 128 * h
                lower = col <= row + o + 8 * t
                g = rows[t][h] * scale
                w_ref[o + 8 * t : o + 8 * t + 8, 128 * h : 128 * h + 128] = jnp.where(lower, g, 0.0)
                g_ref[8 * t : 8 * t + 8, 128 * h : 128 * h + 128] = jnp.where(lower | (col >= end), g, 0.0)
        if end < width:
            first = end // 128 * 128
            g = g_ref[...]
            update = row_dot(g[:, first:], g, HIGHEST)[end - first :]
            col = lax.broadcasted_iota(jnp.int32, (width - end, width), 1)
            old = a_ref[end:, :]
            a_ref[end:, :] = jnp.where((col >= o) & (col < end), 0.0, old) - update


def solve_kernel(packed_ref, psi_ref, occupation_ref, count_ref, orbitals_ref, contribution_ref,
                 psi_v, out_v, a_ref, w_ref, r_ref, g_ref, in_sems, out_sems):
    rows, width = psi_ref.shape
    n = rows // CHUNK
    ins = [
        pltpu.make_async_copy(psi_ref.at[pl.ds(c * CHUNK, CHUNK)], psi_v.at[pl.ds(c * CHUNK, CHUNK)], in_sems.at[c])
        for c in range(n)
    ]
    outs = [
        pltpu.make_async_copy(out_v.at[pl.ds(c * CHUNK, CHUNK)], orbitals_ref.at[pl.ds(c * CHUNK, CHUNK)], out_sems.at[c])
        for c in range(n)
    ]
    for copy in ins:
        copy.start()
    diagonals = [jnp.zeros((1, 128), F32) for _ in range(width // 128)]
    for i in range(width // 8):
        for h in range(width // 128):
            w_ref[8 * i : 8 * i + 8, 128 * h : 128 * h + 128] = packed_ref[17 * i + 8 * h : 17 * i + 8 * h + 8]
        diagonals[8 * i // 128] += packed_ref[17 * i + 16 : 17 * i + 17]
    packed = w_ref[...]
    turned = jnp.transpose(packed)
    row = lax.broadcasted_iota(jnp.int32, (width, width), 0)
    col = lax.broadcasted_iota(jnp.int32, (width, width), 1)
    diagonal = jnp.concatenate(diagonals, axis=1)
    a_ref[...] = jnp.where(row >= col, packed, turned)
    r_ref[...] = jnp.where(row < col, packed, jnp.where(row == col, jnp.broadcast_to(diagonal, packed.shape), turned))
    factor(a_ref, w_ref, g_ref)
    inverse = w_ref[...]
    half = jnp.dot(inverse, r_ref[...], precision=HIGHEST, preferred_element_type=F32)
    projected = lax.dot_general(half, inverse, (((1,), (1,)), ((), ())), precision=HIGHEST, preferred_element_type=F32)
    identity = jnp.where(row == col, 1.0, 0.0)
    rotation = row_dot(inverse, identity - step_size * projected, HIGHEST).astype(BF16)

    state = lax.broadcasted_iota(jnp.int32, (1, width), 1)
    total = 16.0 * width
    weights = occupation_ref[...].astype(F32) * jnp.where(state < count_ref[0], 1.0, 0.0) / (2.0 * total)
    by_state = jnp.transpose(jnp.broadcast_to(weights, (128, width)))
    parts = []
    for c in range(n):
        ins[c].wait()
        for s in range(CHUNK // 256):
            start = c * CHUNK + s * 256
            psi = psi_v[start : start + 256]
            out_v[start : start + 256] = jnp.dot(psi, rotation, preferred_element_type=F32).astype(BF16)
            rotated = lax.dot_general(rotation, psi, (((0,), (1,)), ((), ())), preferred_element_type=F32)
            for h in range(2):
                piece = rotated[:, 128 * h : 128 * h + 128]
                parts.append(jnp.sum(piece * piece * by_state, axis=0, keepdims=True))
        outs[c].start()
    contribution = jnp.concatenate(parts, axis=0)
    for i in range(contribution_ref.shape[0]):
        contribution_ref[i] = contribution
    for copy in outs:
        copy.wait()


def per_device(orbitals, potential, core_density, occupation, slice_counts):
    coefficient = (3.0 / jnp.pi) ** (1.0 / 3.0)
    rows, width = orbitals.shape
    peers = lax.axis_size(GRID)
    groups = lax.axis_size("cuts")
    blocks = rows // 128
    n = rows // CHUNK
    following = lax.ppermute(orbitals[:1], GRID, [((i + 1) % peers, i) for i in range(peers)])
    potential = potential.reshape(blocks, 128)
    gram = pl.pallas_call(
        gram_kernel,
        out_shape=jax.ShapeDtypeStruct((width, 2 * width), F32),
        in_specs=[pl.BlockSpec(memory_space=pl.ANY), pl.BlockSpec(memory_space=pltpu.VMEM)],
        scratch_shapes=[
            pltpu.VMEM((rows + 2 * EDGE, width), BF16),
            pltpu.VMEM((rows, width), BF16),
            pltpu.SemaphoreType.DMA((n,)),
        ],
        name="gram",
    )(orbitals, potential)
    chunk = 17 * 128
    packed = pl.pallas_call(
        pack_kernel, out_shape=jax.ShapeDtypeStruct((17 * width // 8, 128), F32), name="pack"
    )(gram, orbitals[rows - 1 :], following)
    mine = lax.all_to_all(packed.reshape(peers, 1, chunk), GRID, 0, 0, tiled=True)
    summed = mine.sum(axis=0) / (rows * peers)
    every = lax.all_to_all(jnp.broadcast_to(summed[None], (peers, 1, chunk)), GRID, 0, 0, tiled=True)
    orbitals_out, contribution = pl.pallas_call(
        solve_kernel,
        out_shape=(
            jax.ShapeDtypeStruct((rows, width), BF16),
            jax.ShapeDtypeStruct((groups, blocks, 128), F32),
        ),
        in_specs=[
            pl.BlockSpec(memory_space=pltpu.VMEM),
            pl.BlockSpec(memory_space=pl.ANY),
            pl.BlockSpec(memory_space=pltpu.VMEM),
            pl.BlockSpec(memory_space=pltpu.SMEM),
        ],
        out_specs=(pl.BlockSpec(memory_space=pl.ANY), pl.BlockSpec(memory_space=pltpu.VMEM)),
        scratch_shapes=[
            pltpu.VMEM((rows, width), BF16),
            pltpu.VMEM((rows, width), BF16),
            pltpu.VMEM((width, width), F32),
            pltpu.VMEM((width, width), F32),
            pltpu.VMEM((width, width), F32),
            pltpu.VMEM((PANEL, width), F32),
            pltpu.SemaphoreType.DMA((n,)),
            pltpu.SemaphoreType.DMA((n,)),
        ],
        name="solve",
    )(every.reshape(17 * width // 8, 128), orbitals, occupation.reshape(1, width), slice_counts)
    density = core_density.reshape(blocks, 128) + lax.all_to_all(contribution, "cuts", 0, 0, tiled=True).sum(axis=0)
    potential_out = (1.0 - mixing) * potential + mixing * (-coefficient * jnp.cbrt(density))
    return (orbitals_out, potential_out.reshape(rows))


def solution(mesh):
    torus = Mesh(mesh.devices.reshape(mesh.shape["cuts"], 16, 2), ("cuts", "grid_0", "grid_1"))
    in_specs = (P(GRID, "cuts"), P(GRID), P(GRID), P("cuts"), P("cuts"))
    out_specs = (P(GRID, "cuts"), P(GRID))
    return jax.shard_map(
        per_device, mesh=torus, in_specs=in_specs, out_specs=out_specs, check_vma=False
    )
```

time: 194 us -> 113 us (0.58)
  other arithmetic: 57.3 us -> 0.83 us
  starting transfers between devices: 43.1 us -> 17.7 us
  Pallas kernels: 0 us -> 23.2 us
  blocking collectives: 26.4 us -> 46.1 us
  local copies, waits for them, and re-layouts: 21.1 us -> 3.43 us
  waiting for transfers between devices: 34.6 us -> 19.3 us
  matrix products: 7.43 us -> 0 us
    another operation x9 -> x0, other arithmetic: 54.5 us -> none  [the longest x6 33.9 us: per_device(): factor = jnp.linalg.cholesky(intersection)]
    all_to_all x0 -> x2, blocking collectives: none -> 46.1 us  [the longest x1 27.1 us: per_device(): lax.all_to_all(packed.reshape(peers, 1, chunk), GRID, 0, 0, tiled=True)]
    all_gather x2 -> x0, blocking collectives: 26.4 us -> none  [gather_axes(): x = lax.all_gather(x, axis, axis=dim, tiled=True)]
    all_to_all x2 -> x1, starting transfers between devices: 28.3 us -> 4.86 us  [per_device(): lax.all_to_all(jnp.broadcast_to(summed[None], (peers, 1, chunk)), GRID, 0...]
    pallas_call x0 -> x3, Pallas kernels: none -> 23.2 us  [the longest x1 15.8 us: per_device(): pl.pallas_call(solve_kernel, out_shape=(jax.ShapeDtypeStruct((rows, width...]
    all_to_all x2 -> x1, waiting for transfers between devices: 33.9 us -> 19.3 us  [per_device(): lax.all_to_all(jnp.broadcast_to(summed[None], (peers, 1, chunk)), GRID, 0...]
    concatenate x1 -> x0, local copies, waits for them, and re-layouts: 9.22 us -> none  [with_halo(): x = jnp.concatenate([before, x, after], axis=dim)]
    dot_general x5 -> x0, matrix products: 6.12 us -> none  [the longest x1 2.58 us: per_device(): rotated = jnp.dot(orbitals, rotation, preferred_element_type=jnp.float32)]
  transfers between devices with their start and end apart: 4 -> 2, of which waited for: 3 -> 1; matrix products, arithmetic and copies ran while one was open for 2% -> 0% of each run, Pallas kernels for 0% -> 5%
where the time goes in v1:
time: 113 us; the launch traced here: 112 us
  blocking collectives  46.1 us (41%)
  Pallas kernels  23.2 us (21%)
  waiting for transfers between devices  19.3 us (17%)
  starting transfers between devices  17.7 us (16%)
  local copies, waits for them, and re-layouts  3.43 us (3%)
  between operations  1.37 us (1%)
    all_to_all x1, blocking collectives, per_device(): lax.all_to_all(packed.reshape(peers, 1, chunk), GRID, 0, 0, tiled=True)  27.1 us
    all_to_all x1, waiting for transfers between devices, per_device(): lax.all_to_all(jnp.broadcast_to(summed[None], (peers, 1, chunk)), GRID, 0...  19.3 us
    all_to_all x1, blocking collectives, per_device(): lax.all_to_all(contribution, 'cuts', 0, 0, tiled=True).sum(axis=0)  19 us
    pallas_call x1, Pallas kernels, per_device(): pl.pallas_call(solve_kernel, out_shape=(jax.ShapeDtypeStruct((rows, width...  15.8 us
    ppermute x1, starting transfers between devices, per_device(): lax.ppermute(orbitals[:1], GRID, [((i + 1) % peers, i) for i in range(pee...  12.9 us
    pallas_call x1, Pallas kernels, per_device(): pl.pallas_call(gram_kernel, out_shape=jax.ShapeDtypeStruct((width, 2 * wi...  5.44 us
    all_to_all x1, starting transfers between devices, per_device(): lax.all_to_all(jnp.broadcast_to(summed[None], (peers, 1, chunk)), GRID, 0...  4.86 us
  transfers between devices with their start and end apart: 2, of which 1 were waited for; matrix products, arithmetic and copies ran while one was open for 0% of the time, Pallas kernels for 5%

profile of v1, /device:TPU:1, one launch (start us, length us, event | category | flops | bytes accessed | tf_op | source)
XLA Modules:
  0.0 111.9 jit_solution(13356828593014847721)
XLA Ops:
  0.6 1.3 %fusion.3 = (bf16[1,256]{1,0:T(2,128)(2,1)S(1)}, bf16[1,256]{1,0:T(2,128)(2,1)}) fusion(bf16[4096,256]{1,0:T(8,128)(2,1)} %psi_ref.3), kind=kLoop, calls=%fused_computation.5 | loop fusion | bytes 2048 | tf_op jit(solution)/shard_map/slice | solution.py:209
  1.9 12.9 %collective-permute-start = (bf16[1,256]{1,0:T(2,128)(2,1)S(1)}, bf16[1,256]{1,0:T(2,128)(2,1)S(1)}, u32[]{:S(2)}, u32[]{:S(2)}) collective-permute-start(bf16[1,256]{1,0:T(2,128)(2,1)S(1)} %get-tuple-element.6), channel_id=1, source_target_pairs={{1,0},{2,1},{3,2},{4,3},{5,4},{6,5},{7,6},{8,7},{9,8},{10,9},{11,1... | collective-permute-start | bytes 1544 | tf_op jit(solution)/shard_map/ppermute | solution.py:209
  14.8 5.4 %gram.1.gram_ref = f32[256,512]{1,0:T(8,128)} custom-call(bf16[4096,256]{1,0:T(8,128)(2,1)} %psi_ref.3, f32[32,128]{1,0:T(8,128)} %bitcast.14), custom_call_target="tpu_custom_call" | custom-call | tf_op jit(solution)/shard_map/gram/pallas_call | solution.py:211
  20.2 0.0 collective-permute-done.next_ref
  20.2 0.0 copy-start.3
  20.2 0.6 copy-done.3
  20.8 2.0 %pack.1 = f32[544,128]{1,0:T(8,128)} custom-call(f32[256,512]{1,0:T(8,128)} %gram.1.gram_ref, bf16[1,256]{1,0:T(2,128)(2,1)} %get-tuple-element.7.last_ref, bf16[1,256]{1,0:T(2,128)(2,1)} %copy-done.3), custom_call_target="tpu_custom_call" | custom-call | tf_op jit(solution)/shard_map/pack/pallas_call | solution.py:223
  22.8 27.1 %all_to_all.15 = f32[32,1,2176]{2,1,0:T(1,128)S(1)} all-to-all(f32[32,1,2176]{2,1,0:T(1,128)} %bitcast.13), channel_id=1, replica_groups=mesh['cuts'=16,'grid_0'=16,'grid_1'=2] {'grid_0','grid_1'}, dimensions={0} | all-to-all | bytes 557056 | tf_op jit(solution)/shard_map/all_to_all | solution.py:226
  49.9 0.2 reduce_sum.20
  50.1 0.0 copy-start.1
  50.1 0.0 copy-start.2
  50.1 0.9 broadcast_in_dim.2
  51.0 4.9 %all-to-all-start.1 = ((f32[32,1,2176]{2,1,0:T(1,128)}), f32[32,1,2176]{2,1,0:T(1,128)S(1)}, u32[]{:S(2)}, u32[]{:S(2)}) async-start(f32[32,1,2176]{2,1,0:T(1,128)} %broadcast_in_dim.2), calls=%async_computation.1 | async-start | bytes 557056 | tf_op jit(solution)/shard_map/all_to_all | solution.py:228
  56.5 19.3 %all-to-all-done.1 = f32[32,1,2176]{2,1,0:T(1,128)S(1)} async-done(((f32[32,1,2176]{2,1,0:T(1,128)}), f32[32,1,2176]{2,1,0:T(1,128)S(1)}, u32[]{:S(2)}, u32[]{:S(2)}) %all-to-all-start.1) | async-done | bytes 278560 | tf_op jit(solution)/shard_map/all_to_all | solution.py:228
  75.7 0.0 copy-start
  75.7 0.7 copy-done
  76.4 15.8 %solve.1 = (bf16[4096,256]{1,0:T(8,128)(2,1)}, f32[16,32,128]{2,1,0:T(8,128)}) custom-call(f32[544,128]{1,0:T(8,128)} %bitcast.12, bf16[4096,256]{1,0:T(8,128)(2,1)} %psi_ref.3, s32[1,256]{1,0:T(1,128)} %bitcast.15, s32[1]{0:T(128)S(6)} %copy.8.count_ref), custom_call_target="tpu_custom_call" | custom-call | tf_op jit(solution)/shard_map/solve/pallas_call | solution.py:229
  92.2 19.0 %all_to_all.16 = f32[16,32,128]{2,1,0:T(8,128)S(1)} all-to-all(f32[16,32,128]{2,1,0:T(8,128)} %get-tuple-element.5), channel_id=1, replica_groups=mesh['cuts'=16,'grid_0'=16,'grid_1'=2] {'cuts'}, dimensions={0} | all-to-all | bytes 524288 | tf_op jit(solution)/shard_map/all_to_all | solution.py:254
  111.3 0.0 copy-done.1
  111.3 0.0 copy-done.2
  111.3 0.6 fusion.2
  (2 shorter events, 0.0 us)
Async XLA Ops:
  1.9 18.3 %collective-permute-start = (bf16[1,256]{1,0:T(2,128)(2,1)S(1)}, bf16[1,256]{1,0:T(2,128)(2,1)S(1)}, u32[]{:S(2)}, u32[]{:S(2)}) collective-permute-start(bf16[1,256]{1,0:T(2,128)(2,1)S(1)} %get-tuple-element.6), channel_id=1, source_target_pairs={{1,0},{2,1},{3,2},{4,3},{5,4},{6,5},{7,6},{8,7},{9,8},{10,9},{11,1... | collective-permute-start | bytes 1544 | tf_op jit(solution)/shard_map/ppermute | solution.py:209
  20.2 0.6 copy-start.3
  50.1 61.2 %copy-start.1 = (f32[4096]{0:T(1024)S(1)}, f32[4096]{0:T(1024)}, u32[]{:S(2)}) copy-start(f32[4096]{0:T(1024)} %param.6) | copy-start | bytes 49156
  50.1 61.2 %copy-start.2 = (f32[4096]{0:T(1024)S(1)}, f32[4096]{0:T(1024)}, u32[]{:S(2)}) copy-start(f32[4096]{0:T(1024)} %param.7) | copy-start | bytes 49156
  51.0 24.8 %all-to-all-start.1 = ((f32[32,1,2176]{2,1,0:T(1,128)}), f32[32,1,2176]{2,1,0:T(1,128)S(1)}, u32[]{:S(2)}, u32[]{:S(2)}) async-start(f32[32,1,2176]{2,1,0:T(1,128)} %broadcast_in_dim.2), calls=%async_computation.1 | async-start | bytes 557056 | tf_op jit(solution)/shard_map/all_to_all | solution.py:228
  75.7 0.7 copy-start

commit v2 on v1

v2 whole, which is shorter than its diff:
```python
import functools

import jax
import jax.numpy as jnp
from jax import lax
from jax.experimental import pallas as pl
from jax.experimental.pallas import tpu as pltpu
from jax.sharding import Mesh
from jax.sharding import PartitionSpec as P

GRID = ("grid_0", "grid_1")
HIGHEST = lax.Precision.HIGHEST
F32 = jnp.float32
BF16 = jnp.bfloat16

mixing = 0.3
step_size = 0.5

PANEL = 64
CHUNK = 1024
PIECE = 2048
EDGE = 16


def row_dot(a, b, precision=None):
    return lax.dot_general(a, b, (((0,), (0,)), ((), ())), precision=precision, preferred_element_type=F32)


def gram_kernel(psi_ref, potential_ref, out_ref, last_ref, psi_v, applied_v, sems):
    rows, width = psi_ref.shape
    n = rows // CHUNK
    copies = [
        pltpu.make_async_copy(
            psi_ref.at[pl.ds(c * CHUNK, CHUNK)], psi_v.at[pl.ds(EDGE + c * CHUNK, CHUNK)], sems.at[c]
        )
        for c in range(n)
    ]
    for copy in copies:
        copy.start()
    psi_v[0:EDGE] = jnp.zeros((EDGE, width), BF16)
    psi_v[EDGE + rows : EDGE + rows + EDGE] = jnp.zeros((EDGE, width), BF16)
    by_row = jnp.transpose(potential_ref[...])
    intersection = ritz = None
    copies[0].wait()
    for c in range(n + 1):
        if c + 1 < n:
            copies[c + 1].wait()
        if c < n:
            for s in range(CHUNK // 128):
                start = c * CHUNK + s * 128
                block = start // 128
                wide = psi_v[start : start + 128 + 2 * EDGE].astype(F32)
                length = wide.shape[0]
                after = pltpu.roll(wide, length - 1, 0)[EDGE : EDGE + 128]
                before = pltpu.roll(wide, 1, 0)[EDGE : EDGE + 128]
                middle = wide[EDGE : EDGE + 128]
                kinetic = -0.5 * (after + before - 2.0 * middle)
                applied_v[start : start + 128] = (kinetic + by_row[:, block : block + 1] * middle).astype(BF16)
            psi = psi_v[EDGE + c * CHUNK : EDGE + (c + 1) * CHUNK]
            one = row_dot(psi, psi)
            intersection = one if c == 0 else intersection + one
        if c > 0:
            psi = psi_v[EDGE + (c - 1) * CHUNK : EDGE + c * CHUNK]
            one = row_dot(psi, applied_v[(c - 1) * CHUNK : c * CHUNK])
            ritz = one if c == 1 else ritz + one
    row = lax.broadcasted_iota(jnp.int32, (8, 128), 0)
    col = lax.broadcasted_iota(jnp.int32, (8, 128), 1)
    for i in range(width // 8):
        for h in range(width // 128):
            one = intersection[8 * i : 8 * i + 8, 128 * h : 128 * h + 128]
            two = ritz[8 * i : 8 * i + 8, 128 * h : 128 * h + 128]
            out_ref[17 * i + 8 * h : 17 * i + 8 * h + 8] = jnp.where(row + 8 * i >= col + 128 * h, one, two)
            if 8 * i // 128 == h:
                diagonal = jnp.sum(jnp.where(row + 8 * i == col + 128 * h, two, 0.0), axis=0, keepdims=True)
        out_ref[17 * i + 16 : 17 * i + 17] = diagonal
    last_ref[...] = psi_v[rows : rows + EDGE]


def border_kernel(packed_ref, last_ref, next_ref, out_ref):
    width = last_ref.shape[1]
    zeros = jnp.zeros((14, width), F32)
    last, following = last_ref[...].astype(F32)[EDGE - 1 :], next_ref[...].astype(F32)[:1]
    left = jnp.concatenate([last, following, zeros], axis=0).astype(BF16)
    right = jnp.concatenate([following, last, zeros], axis=0).astype(BF16)
    across = -0.5 * row_dot(left, right)
    row = lax.broadcasted_iota(jnp.int32, (8, 128), 0)
    col = lax.broadcasted_iota(jnp.int32, (8, 128), 1)
    for i in range(width // 8):
        for h in range(width // 128):
            place = slice(17 * i + 8 * h, 17 * i + 8 * h + 8)
            piece = across[8 * i : 8 * i + 8, 128 * h : 128 * h + 128]
            if 8 * i >= 128 * (h + 1):
                out_ref[place] = packed_ref[place]
            else:
                out_ref[place] = packed_ref[place] + jnp.where(row + 8 * i < col + 128 * h, piece, 0.0)
            if 8 * i // 128 == h:
                diagonal = jnp.sum(jnp.where(row + 8 * i == col + 128 * h, piece, 0.0), axis=0, keepdims=True)
        place = slice(17 * i + 16, 17 * i + 17)
        out_ref[place] = packed_ref[place] + diagonal


def spread_kernel(points, arrived_ref, out_ref):
    peers = arrived_ref.shape[0]
    total = arrived_ref[0]
    for i in range(1, peers):
        total = total + arrived_ref[i]
    total = total * (1.0 / points)
    for i in range(peers):
        out_ref[i] = total


def eliminate(rows, base):
    n = len(rows)
    row = lax.broadcasted_iota(jnp.int32, (8, 128), 0)
    lane = lax.broadcasted_iota(jnp.int32, (8, 128), 1)
    pivots = []

    def columns(t, c, count):
        h, l = c // 128, c % 128
        return [jnp.broadcast_to(rows[t][h][:, l + j : l + j + 1], (8, 128)) for j in range(count)]

    def replaced(t, c, diagonal):
        h, l = c // 128, c % 128
        inside = (lane >= l) & (lane < l + 8)
        rows[t][h] = jnp.where(inside, jnp.where(lane - l == row, 1.0, 0.0) if diagonal else 0.0, rows[t][h])

    for p in range(0, n, 2):
        c = base + 8 * p
        cols = [columns(p + q, c, 16) for q in range(2)]
        replaced(p, c, True)
        replaced(p + 1, c, False)
        steps = []
        for k in range(16):
            q, m = k // 8, k % 8
            spread = lambda v: jnp.broadcast_to(v[m : m + 1, :], (8, 128))
            if k == 8:
                replaced(p + 1, c + 8, True)
            d = spread(cols[q][k])
            pivot = d if m == 0 else jnp.where(row >= m, d, pivot)
            r = 1.0 / d
            above = {j: spread(cols[q][j]) for j in range(k + 1, 16)}
            pivot_row = [spread(rows[p + q][s]) for s in range(2)]
            steps.append((r, above, pivot_row))
            for i in range(q, 2):
                if i == q and m == 7:
                    continue
                f = cols[i][k] * r
                if i == q:
                    f = jnp.where(row > m, f, 0.0)
                for j in range(k + 1, 16):
                    cols[i][j] = cols[i][j] - f * above[j]
                for s in range(2):
                    rows[p + i][s] = rows[p + i][s] - f * pivot_row[s]
            if m == 7:
                pivots.append(pivot)
        for t in range(p + 2, n):
            for q in range(2):
                mine = columns(t, c + 8 * q, 8)
                replaced(t, c + 8 * q, False)
                for m in range(8):
                    r, above, pivot_row = steps[8 * q + m]
                    f = mine[m] * r
                    for j in range(m + 1, 8):
                        mine[j] = mine[j] - f * above[8 * q + j]
                    for s in range(2):
                        rows[t][s] = rows[t][s] - f * pivot_row[s]
    return rows, pivots


def factor(a_ref, w_ref, g_ref):
    row = lax.broadcasted_iota(jnp.int32, (8, 128), 0)
    lane = lax.broadcasted_iota(jnp.int32, (8, 128), 1)
    width = a_ref.shape[0]
    for o in range(0, width, PANEL):
        end = o + PANEL
        rows = [[a_ref[o + 8 * t : o + 8 * t + 8, 128 * h : 128 * h + 128] for h in range(2)] for t in range(PANEL // 8)]
        rows, pivots = eliminate(rows, o)
        for t in range(PANEL // 8):
            scale = lax.rsqrt(pivots[t])
            for h in range(2):
                col = lane + 128 * h
                lower = col <= row + o + 8 * t
                g = rows[t][h] * scale
                w_ref[o + 8 * t : o + 8 * t + 8, 128 * h : 128 * h + 128] = jnp.where(lower, g, 0.0)
                g_ref[8 * t : 8 * t + 8, 128 * h : 128 * h + 128] = jnp.where(lower | (col >= end), g, 0.0)
        if end < width:
            first = end // 128 * 128
            g = g_ref[...]
            update = row_dot(g[:, first:], g, HIGHEST)[end - first :]
            col = lax.broadcasted_iota(jnp.int32, (width - end, width), 1)
            old = a_ref[end:, :]
            a_ref[end:, :] = jnp.where((col >= o) & (col < end), 0.0, old) - update


def solve_kernel(packed_ref, psi_ref, occupation_ref, count_ref, orbitals_ref, contribution_ref,
                 psi_v, out_v, a_ref, w_ref, r_ref, g_ref, in_sems, out_sems):
    rows, width = psi_ref.shape
    n = rows // PIECE
    ins = [
        pltpu.make_async_copy(psi_ref.at[pl.ds(c * PIECE, PIECE)], psi_v.at[pl.ds(c * PIECE, PIECE)], in_sems.at[c])
        for c in range(n)
    ]
    outs = [
        pltpu.make_async_copy(out_v.at[pl.ds(c * PIECE, PIECE)], orbitals_ref.at[pl.ds(c * PIECE, PIECE)], out_sems.at[c])
        for c in range(n)
    ]
    for copy in ins:
        copy.start()
    diagonals = [jnp.zeros((1, 128), F32) for _ in range(width // 128)]
    for i in range(width // 8):
        for h in range(width // 128):
            w_ref[8 * i : 8 * i + 8, 128 * h : 128 * h + 128] = packed_ref[17 * i + 8 * h : 17 * i + 8 * h + 8]
        diagonals[8 * i // 128] += packed_ref[17 * i + 16 : 17 * i + 17]
    packed = w_ref[...]
    turned = jnp.transpose(packed)
    row = lax.broadcasted_iota(jnp.int32, (width, width), 0)
    col = lax.broadcasted_iota(jnp.int32, (width, width), 1)
    diagonal = jnp.concatenate(diagonals, axis=1)
    a_ref[...] = jnp.where(row >= col, packed, turned)
    r_ref[...] = jnp.where(row < col, packed, jnp.where(row == col, jnp.broadcast_to(diagonal, packed.shape), turned))
    factor(a_ref, w_ref, g_ref)
    inverse = w_ref[...]
    half = jnp.dot(inverse, r_ref[...], precision=HIGHEST, preferred_element_type=F32)
    projected = lax.dot_general(half, inverse, (((1,), (1,)), ((), ())), precision=HIGHEST, preferred_element_type=F32)
    identity = jnp.where(row == col, 1.0, 0.0)
    rotation = row_dot(inverse, identity - step_size * projected, HIGHEST).astype(BF16)

    state = lax.broadcasted_iota(jnp.int32, (1, width), 1)
    total = 16.0 * width
    weights = occupation_ref[...].astype(F32) * jnp.where(state < count_ref[...], 1.0, 0.0) / (2.0 * total)
    on_diagonal = lax.broadcasted_iota(jnp.int32, (128, 128), 0) == lax.broadcasted_iota(jnp.int32, (128, 128), 1)
    parts = []
    for c in range(n):
        ins[c].wait()
        for s in range(PIECE // 256):
            start = c * PIECE + s * 256
            rotated = jnp.dot(psi_v[start : start + 256], rotation, preferred_element_type=F32)
            out_v[start : start + 256] = rotated.astype(BF16)
            weighted = rotated * rotated * weights
            weighted = weighted[:, :128] + weighted[:, 128:]
            for h in range(2):
                sums = jnp.sum(weighted[128 * h : 128 * h + 128], axis=1, keepdims=True)
                parts.append(jnp.sum(jnp.where(on_diagonal, sums, 0.0), axis=0, keepdims=True))
        outs[c].start()
    contribution = jnp.concatenate(parts, axis=0)
    for i in range(contribution_ref.shape[0]):
        contribution_ref[i] = contribution
    for copy in outs:
        copy.wait()


def in_vmem(x):
    return pltpu.with_memory_space_constraint(x, pltpu.VMEM)


def per_device(orbitals, potential, core_density, occupation, slice_counts):
    coefficient = (3.0 / jnp.pi) ** (1.0 / 3.0)
    rows, width = orbitals.shape
    peers = lax.axis_size(GRID)
    groups = lax.axis_size("cuts")
    blocks = rows // 128
    n = rows // CHUNK
    following = lax.ppermute(orbitals[:8], GRID, [((i + 1) % peers, i) for i in range(peers)])
    potential = potential.reshape(blocks, 128)
    packed, last = pl.pallas_call(
        gram_kernel,
        out_shape=(pltpu.VMEM((17 * width // 8, 128), F32), pltpu.VMEM((EDGE, width), BF16)),
        in_specs=[pl.BlockSpec(memory_space=pl.ANY), pl.BlockSpec(memory_space=pltpu.VMEM)],
        scratch_shapes=[
            pltpu.VMEM((rows + 2 * EDGE, width), BF16),
            pltpu.VMEM((rows, width), BF16),
            pltpu.SemaphoreType.DMA((n,)),
        ],
        name="gram",
    )(orbitals, potential)
    chunk = 17 * 128
    packed = pl.pallas_call(border_kernel, out_shape=pltpu.VMEM((17 * width // 8, 128), F32), name="border")(
        in_vmem(packed), in_vmem(last), in_vmem(following)
    )
    mine = lax.all_to_all(packed.reshape(peers, 1, chunk), GRID, 0, 0, tiled=True)
    copies = pl.pallas_call(functools.partial(spread_kernel, rows * peers), out_shape=pltpu.VMEM((peers, 1, chunk), F32), name="spread")(in_vmem(mine))
    every = lax.all_to_all(copies, GRID, 0, 0, tiled=True)
    orbitals_out, contribution = pl.pallas_call(
        solve_kernel,
        out_shape=(
            jax.ShapeDtypeStruct((rows, width), BF16),
            pltpu.VMEM((groups, blocks, 128), F32),
        ),
        in_specs=[
            pl.BlockSpec(memory_space=pltpu.VMEM),
            pl.BlockSpec(memory_space=pl.ANY),
            pl.BlockSpec(memory_space=pltpu.VMEM),
            pl.BlockSpec(memory_space=pltpu.VMEM),
        ],
        out_specs=(pl.BlockSpec(memory_space=pl.ANY), pl.BlockSpec(memory_space=pltpu.VMEM)),
        scratch_shapes=[
            pltpu.VMEM((rows, width), BF16),
            pltpu.VMEM((rows, width), BF16),
            pltpu.VMEM((width, width), F32),
            pltpu.VMEM((width, width), F32),
            pltpu.VMEM((width, width), F32),
            pltpu.VMEM((PANEL, width), F32),
            pltpu.SemaphoreType.DMA((rows // PIECE,)),
            pltpu.SemaphoreType.DMA((rows // PIECE,)),
        ],
        name="solve",
    )(in_vmem(every.reshape(17 * width // 8, 128)), orbitals, occupation.reshape(1, width), slice_counts.reshape(1, 1))
    density = core_density.reshape(blocks, 128) + lax.all_to_all(contribution, "cuts", 0, 0, tiled=True).sum(axis=0)
    potential_out = (1.0 - mixing) * potential + mixing * (-coefficient * jnp.cbrt(density))
    return (orbitals_out, potential_out.reshape(rows))


def solution(mesh):
    torus = Mesh(mesh.devices.reshape(mesh.shape["cuts"], 16, 2), ("cuts", "grid_0", "grid_1"))
    in_specs = (P(GRID, "cuts"), P(GRID), P(GRID), P("cuts"), P("cuts"))
    out_specs = (P(GRID, "cuts"), P(GRID))
    return jax.shard_map(
        per_device, mesh=torus, in_specs=in_specs, out_specs=out_specs, check_vma=False
    )
```

time: 113 us -> 103 us (0.912)
  Pallas kernels: 23.2 us -> 17.4 us
  local copies, waits for them, and re-layouts: 3.43 us -> 0.7 us
    pallas_call x1, Pallas kernels: 15.8 us -> 11.7 us  [per_device(): pl.pallas_call(solve_kernel, out_shape=(jax.ShapeDtypeStruct((rows, width...]
    pallas_call x2 -> x3, Pallas kernels: 7.44 us -> 5.75 us  [the longest x1 4.74 us: per_device(): pl.pallas_call(gram_kernel, out_shape=(pltpu.VMEM((17 * width // 8, 128),...]
    unnamed x8 -> x4, local copies, waits for them, and re-layouts: 1.29 us -> 0.01 us
where the time goes in v2:
time: 103 us
  blocking collectives  46.1 us (45%)
  waiting for transfers between devices  19.1 us (19%)
  starting transfers between devices  17.5 us (17%)
  Pallas kernels  17.4 us (17%)
  between operations  1.34 us (1%)
    all_to_all x1, blocking collectives, per_device(): lax.all_to_all(packed.reshape(peers, 1, chunk), GRID, 0, 0, tiled=True)  26.9 us
    all_to_all x1, blocking collectives, per_device(): lax.all_to_all(contribution, 'cuts', 0, 0, tiled=True).sum(axis=0)  19.2 us
    all_to_all x1, waiting for transfers between devices, per_device(): every = lax.all_to_all(copies, GRID, 0, 0, tiled=True)  19.1 us
    ppermute x1, starting transfers between devices, per_device(): lax.ppermute(orbitals[:8], GRID, [((i + 1) % peers, i) for i in range(pee...  12.9 us
    pallas_call x1, Pallas kernels, per_device(): pl.pallas_call(solve_kernel, out_shape=(jax.ShapeDtypeStruct((rows, width...  11.7 us
    pallas_call x1, Pallas kernels, per_device(): pl.pallas_call(gram_kernel, out_shape=(pltpu.VMEM((17 * width // 8, 128),...  4.74 us
    all_to_all x1, starting transfers between devices, per_device(): every = lax.all_to_all(copies, GRID, 0, 0, tiled=True)  4.67 us
  transfers between devices with their start and end apart: 2, of which 1 were waited for; matrix products, arithmetic and copies ran while one was open for 0% of the time, Pallas kernels for 5%

profile of v2, /device:TPU:1, one launch (start us, length us, event | category | flops | bytes accessed | tf_op | source)
XLA Modules:
  0.0 102.9 jit_solution(3084148379633899067)
XLA Ops:
  0.6 0.7 slice.3
  1.3 12.9 %collective-permute-start = (bf16[8,256]{1,0:T(8,128)(2,1)S(1)}, bf16[8,256]{1,0:T(8,128)(2,1)S(1)}, u32[]{:S(2)}, u32[]{:S(2)}) collective-permute-start(bf16[8,256]{1,0:T(8,128)(2,1)S(1)} %slice.3), channel_id=1, source_target_pairs={{1,0},{2,1},{3,2},{4,3},{5,4},{6,5},{7,6},{8,7},{9,8},{10,9},{11,1... | collective-permute-start | bytes 12296 | tf_op jit(solution)/shard_map/ppermute | solution.py:263
  14.2 4.7 %gram.1 = (f32[544,128]{1,0:T(8,128)S(1)}, bf16[16,256]{1,0:T(8,128)(2,1)S(1)}) custom-call(bf16[4096,256]{1,0:T(8,128)(2,1)} %psi_ref.3, f32[32,128]{1,0:T(8,128)} %bitcast.16), custom_call_target="tpu_custom_call" | custom-call | tf_op jit(solution)/shard_map/gram/pallas_call | solution.py:265
  18.9 0.0 collective-permute-done.next_ref
  18.9 0.2 border.1
  19.2 26.9 %all_to_all.15.arrived_ref = f32[32,1,2176]{2,1,0:T(1,128)S(1)} all-to-all(f32[32,1,2176]{2,1,0:T(1,128)S(1)} %bitcast.15), channel_id=1, replica_groups=mesh['cuts'=16,'grid_0'=16,'grid_1'=2] {'grid_0','grid_1'}, dimensions={0} | all-to-all | bytes 557056 | tf_op jit(solution)/shard_map/all_to_all | solution.py:280
  46.1 0.0 copy-start
  46.1 0.0 copy-start.1
  46.1 0.8 spread.1
  46.9 4.7 %all-to-all-start.1 = ((f32[32,1,2176]{2,1,0:T(1,128)}), f32[32,1,2176]{2,1,0:T(1,128)S(1)}, u32[]{:S(2)}, u32[]{:S(2)}) async-start(f32[32,1,2176]{2,1,0:T(1,128)} %spread.1), calls=%async_computation.1 | async-start | bytes 557056 | tf_op jit(solution)/shard_map/all_to_all | solution.py:282
  52.2 19.1 %all-to-all-done.1 = f32[32,1,2176]{2,1,0:T(1,128)S(1)} async-done(((f32[32,1,2176]{2,1,0:T(1,128)}), f32[32,1,2176]{2,1,0:T(1,128)S(1)}, u32[]{:S(2)}, u32[]{:S(2)}) %all-to-all-start.1) | async-done | bytes 278560 | tf_op jit(solution)/shard_map/all_to_all | solution.py:282
  71.3 11.7 %solve.1 = (bf16[4096,256]{1,0:T(8,128)(2,1)}, f32[16,32,128]{2,1,0:T(8,128)S(1)}) custom-call(f32[544,128]{1,0:T(8,128)S(1)} %bitcast.14, bf16[4096,256]{1,0:T(8,128)(2,1)} %psi_ref.3, s32[1,256]{1,0:T(1,128)} %bitcast.17, s32[1,1]{1,0:T(1,128)} %bitcast.13.count_ref), custom_call_target="tpu_custom_call" | custom-call | tf_op jit(solution)/shard_map/solve/pallas_call | solution.py:283
  83.0 19.2 %all_to_all.16 = f32[16,32,128]{2,1,0:T(8,128)S(1)} all-to-all(f32[16,32,128]{2,1,0:T(8,128)S(1)} %get-tuple-element.9), channel_id=1, replica_groups=mesh['cuts'=16,'grid_0'=16,'grid_1'=2] {'cuts'}, dimensions={0} | all-to-all | bytes 524288 | tf_op jit(solution)/shard_map/all_to_all | solution.py:308
  102.2 0.0 copy-done
  102.2 0.0 copy-done.1
  102.2 0.6 fusion.2
  (1 shorter events, 0.0 us)
Async XLA Ops:
  1.3 17.6 %collective-permute-start = (bf16[8,256]{1,0:T(8,128)(2,1)S(1)}, bf16[8,256]{1,0:T(8,128)(2,1)S(1)}, u32[]{:S(2)}, u32[]{:S(2)}) collective-permute-start(bf16[8,256]{1,0:T(8,128)(2,1)S(1)} %slice.3), channel_id=1, source_target_pairs={{1,0},{2,1},{3,2},{4,3},{5,4},{6,5},{7,6},{8,7},{9,8},{10,9},{11,1... | collective-permute-start | bytes 12296 | tf_op jit(solution)/shard_map/ppermute | solution.py:263
  46.1 56.1 %copy-start = (f32[4096]{0:T(1024)S(1)}, f32[4096]{0:T(1024)}, u32[]{:S(2)}) copy-start(f32[4096]{0:T(1024)} %param.6) | copy-start | bytes 49156
  46.1 56.1 %copy-start.1 = (f32[4096]{0:T(1024)S(1)}, f32[4096]{0:T(1024)}, u32[]{:S(2)}) copy-start(f32[4096]{0:T(1024)} %param.7) | copy-start | bytes 49156
  46.9 24.5 %all-to-all-start.1 = ((f32[32,1,2176]{2,1,0:T(1,128)}), f32[32,1,2176]{2,1,0:T(1,128)S(1)}, u32[]{:S(2)}, u32[]{:S(2)}) async-start(f32[32,1,2176]{2,1,0:T(1,128)} %spread.1), calls=%async_computation.1 | async-start | bytes 557056 | tf_op jit(solution)/shard_map/all_to_all | solution.py:282

commit v3 on v2

--- a/solution.py
+++ b/solution.py
@@ -26,41 +26,37 @@
     return lax.dot_general(a, b, (((0,), (0,)), ((), ())), precision=precision, preferred_element_type=F32)
 
 
-def gram_kernel(psi_ref, potential_ref, out_ref, last_ref, psi_v, applied_v, sems):
+def gram_kernel(total_states, psi_ref, potential_ref, occupation_ref, count_ref, out_ref, last_ref, weights_ref, applied_v):
     rows, width = psi_ref.shape
     n = rows // CHUNK
-    copies = [
-        pltpu.make_async_copy(
-            psi_ref.at[pl.ds(c * CHUNK, CHUNK)], psi_v.at[pl.ds(EDGE + c * CHUNK, CHUNK)], sems.at[c]
-        )
-        for c in range(n)
-    ]
-    for copy in copies:
-        copy.start()
-    psi_v[0:EDGE] = jnp.zeros((EDGE, width), BF16)
-    psi_v[EDGE + rows : EDGE + rows + EDGE] = jnp.zeros((EDGE, width), BF16)
+    state = lax.broadcasted_iota(jnp.int32, (1, width), 1)
+    live = jnp.where(state < count_ref[...], 1.0, 0.0)
+    weights_ref[...] = occupation_ref[...].astype(F32) * live / (2.0 * total_states)
     by_row = jnp.transpose(potential_ref[...])
+    outside = jnp.zeros((EDGE, width), BF16)
     intersection = ritz = None
-    copies[0].wait()
     for c in range(n + 1):
-        if c + 1 < n:
-            copies[c + 1].wait()
         if c < n:
             for s in range(CHUNK // 128):
                 start = c * CHUNK + s * 128
                 block = start // 128
-                wide = psi_v[start : start + 128 + 2 * EDGE].astype(F32)
+                if start == 0:
+                    wide = jnp.concatenate([outside, psi_ref[0 : 128 + EDGE]], axis=0).astype(F32)
+                elif start + 128 == rows:
+                    wide = jnp.concatenate([psi_ref[start - EDGE : rows], outside], axis=0).astype(F32)
+                else:
+                    wide = psi_ref[start - EDGE : start + 128 + EDGE].astype(F32)
                 length = wide.shape[0]
                 after = pltpu.roll(wide, length - 1, 0)[EDGE : EDGE + 128]
                 before = pltpu.roll(wide, 1, 0)[EDGE : EDGE + 128]
                 middle = wide[EDGE : EDGE + 128]
                 kinetic = -0.5 * (after + before - 2.0 * middle)
                 applied_v[start : start + 128] = (kinetic + by_row[:, block : block + 1] * middle).astype(BF16)
-            psi = psi_v[EDGE + c * CHUNK : EDGE + (c + 1) * CHUNK]
+            psi = psi_ref[c * CHUNK : (c + 1) * CHUNK]
             one = row_dot(psi, psi)
             intersection = one if c == 0 else intersection + one
         if c > 0:
-            psi = psi_v[EDGE + (c - 1) * CHUNK : EDGE + c * CHUNK]
+            psi = psi_ref[(c - 1) * CHUNK : c * CHUNK]
             one = row_dot(psi, applied_v[(c - 1) * CHUNK : c * CHUNK])
             ritz = one if c == 1 else ritz + one
     row = lax.broadcasted_iota(jnp.int32, (8, 128), 0)
@@ -73,7 +69,7 @@
             if 8 * i // 128 == h:
                 diagonal = jnp.sum(jnp.where(row + 8 * i == col + 128 * h, two, 0.0), axis=0, keepdims=True)
         out_ref[17 * i + 16 : 17 * i + 17] = diagonal
-    last_ref[...] = psi_v[rows : rows + EDGE]
+    last_ref[...] = psi_ref[rows - EDGE : rows]
 
 
 def border_kernel(packed_ref, last_ref, next_ref, out_ref):
@@ -145,10 +141,13 @@
                 if i == q and m == 7:
                     continue
                 f = cols[i][k] * r
+                for j in range(k + 1, 16):
+                    if j == k + 1:
+                        cols[i][j] = cols[i][j] - cols[i][k] * above[j] * r
+                    else:
+                        cols[i][j] = cols[i][j] - f * above[j]
                 if i == q:
                     f = jnp.where(row > m, f, 0.0)
-                for j in range(k + 1, 16):
-                    cols[i][j] = cols[i][j] - f * above[j]
                 for s in range(2):
                     rows[p + i][s] = rows[p + i][s] - f * pivot_row[s]
             if m == 7:
@@ -184,15 +183,16 @@
                 w_ref[o + 8 * t : o + 8 * t + 8, 128 * h : 128 * h + 128] = jnp.where(lower, g, 0.0)
                 g_ref[8 * t : 8 * t + 8, 128 * h : 128 * h + 128] = jnp.where(lower | (col >= end), g, 0.0)
         if end < width:
-            first = end // 128 * 128
             g = g_ref[...]
-            update = row_dot(g[:, first:], g, HIGHEST)[end - first :]
-            col = lax.broadcasted_iota(jnp.int32, (width - end, width), 1)
-            old = a_ref[end:, :]
-            a_ref[end:, :] = jnp.where((col >= o) & (col < end), 0.0, old) - update
-
-
-def solve_kernel(packed_ref, psi_ref, occupation_ref, count_ref, orbitals_ref, contribution_ref,
+            bounds = (end, end + PANEL, width) if end + PANEL < width else (end, width)
+            for low, high in zip(bounds, bounds[1:]):
+                first, last = low // 128 * 128, -(-high // 128) * 128
+                update = row_dot(g[:, first:last], g, HIGHEST)[low - first : high - first]
+                col = lax.broadcasted_iota(jnp.int32, (high - low, width), 1)
+                a_ref[low:high, :] = jnp.where((col >= o) & (col < end), 0.0, a_ref[low:high, :]) - update
+
+
+def solve_kernel(packed_ref, psi_ref, weights_ref, orbitals_ref, contribution_ref,
                  psi_v, out_v, a_ref, w_ref, r_ref, g_ref, in_sems, out_sems):
     rows, width = psi_ref.shape
     n = rows // PIECE
@@ -225,9 +225,7 @@
     identity = jnp.where(row == col, 1.0, 0.0)
     rotation = row_dot(inverse, identity - step_size * projected, HIGHEST).astype(BF16)
 
-    state = lax.broadcasted_iota(jnp.int32, (1, width), 1)
-    total = 16.0 * width
-    weights = occupation_ref[...].astype(F32) * jnp.where(state < count_ref[...], 1.0, 0.0) / (2.0 * total)
+    weights = weights_ref[...]
     on_diagonal = lax.broadcasted_iota(jnp.int32, (128, 128), 0) == lax.broadcasted_iota(jnp.int32, (128, 128), 1)
     parts = []
     for c in range(n):
@@ -259,20 +257,18 @@
     peers = lax.axis_size(GRID)
     groups = lax.axis_size("cuts")
     blocks = rows // 128
-    n = rows // CHUNK
     following = lax.ppermute(orbitals[:8], GRID, [((i + 1) % peers, i) for i in range(peers)])
     potential = potential.reshape(blocks, 128)
-    packed, last = pl.pallas_call(
-        gram_kernel,
-        out_shape=(pltpu.VMEM((17 * width // 8, 128), F32), pltpu.VMEM((EDGE, width), BF16)),
-        in_specs=[pl.BlockSpec(memory_space=pl.ANY), pl.BlockSpec(memory_space=pltpu.VMEM)],
-        scratch_shapes=[
-            pltpu.VMEM((rows + 2 * EDGE, width), BF16),
-            pltpu.VMEM((rows, width), BF16),
-            pltpu.SemaphoreType.DMA((n,)),
-        ],
+    packed, last, weights = pl.pallas_call(
+        functools.partial(gram_kernel, width * groups),
+        out_shape=(
+            pltpu.VMEM((17 * width // 8, 128), F32),
+            pltpu.VMEM((EDGE, width), BF16),
+            pltpu.VMEM((1, width), F32),
+        ),
+        scratch_shapes=[pltpu.VMEM((rows, width), BF16)],
         name="gram",
-    )(orbitals, potential)
+    )(in_vmem(orbitals), potential, occupation.reshape(1, width), slice_counts.reshape(1, 1))
     chunk = 17 * 128
     packed = pl.pallas_call(border_kernel, out_shape=pltpu.VMEM((17 * width // 8, 128), F32), name="border")(
         in_vmem(packed), in_vmem(last), in_vmem(following)
@@ -290,7 +286,6 @@
             pl.BlockSpec(memory_space=pltpu.VMEM),
             pl.BlockSpec(memory_space=pl.ANY),
             pl.BlockSpec(memory_space=pltpu.VMEM),
-            pl.BlockSpec(memory_space=pltpu.VMEM),
         ],
         out_specs=(pl.BlockSpec(memory_space=pl.ANY), pl.BlockSpec(memory_space=pltpu.VMEM)),
         scratch_shapes=[
@@ -304,7 +299,7 @@
             pltpu.SemaphoreType.DMA((rows // PIECE,)),
         ],
         name="solve",
-    )(in_vmem(every.reshape(17 * width // 8, 128)), orbitals, occupation.reshape(1, width), slice_counts.reshape(1, 1))
+    )(in_vmem(every.reshape(17 * width // 8, 128)), orbitals, in_vmem(weights))
     density = core_density.reshape(blocks, 128) + lax.all_to_all(contribution, "cuts", 0, 0, tiled=True).sum(axis=0)
     potential_out = (1.0 - mixing) * potential + mixing * (-coefficient * jnp.cbrt(density))
     return (orbitals_out, potential_out.reshape(rows))

time: 103 us -> 102 us (level)
  blocking collectives: 46.1 us -> 70.3 us
  waiting for transfers between devices: 19.1 us -> 0.01 us
  starting transfers between devices: 17.5 us -> 12.9 us
  Pallas kernels: 17.4 us -> 14.3 us
  local copies, waits for them, and re-layouts: 0.7 us -> 2.28 us
    all_to_all x0 -> x1, blocking collectives: none -> 25.3 us  [per_device(): every = lax.all_to_all(copies, GRID, 0, 0, tiled=True)]
    all_to_all x1 -> x0, waiting for transfers between devices: 19.1 us -> none  [per_device(): every = lax.all_to_all(copies, GRID, 0, 0, tiled=True)]
    all_to_all x1 -> x0, starting transfers between devices: 4.67 us -> none  [per_device(): every = lax.all_to_all(copies, GRID, 0, 0, tiled=True)]
    unnamed x4 -> x6, local copies, waits for them, and re-layouts: 0.01 us -> 1.59 us
    pallas_call x1, Pallas kernels: 4.74 us -> 3.25 us  [per_device(): pl.pallas_call(functools.partial(gram_kernel, width * groups), out_shape=...]
    all_to_all x1, blocking collectives: 19.2 us -> 18.1 us  [per_device(): lax.all_to_all(contribution, 'cuts', 0, 0, tiled=True).sum(axis=0)]
  transfers between devices with their start and end apart: 2 -> 1, of which waited for: 1 -> 0; matrix products, arithmetic and copies ran while one was open for 0% -> 0% of each run, Pallas kernels for 5% -> 3%
where the time goes in v3:
time: 102 us
  blocking collectives  70.3 us (69%)
  Pallas kernels  14.3 us (14%)
  starting transfers between devices  12.9 us (13%)
  local copies, waits for them, and re-layouts  2.28 us (2%)
  between operations  1.34 us (1%)
    all_to_all x1, blocking collectives, per_device(): lax.all_to_all(packed.reshape(peers, 1, chunk), GRID, 0, 0, tiled=True)  26.9 us
    all_to_all x1, blocking collectives, per_device(): every = lax.all_to_all(copies, GRID, 0, 0, tiled=True)  25.3 us
    all_to_all x1, blocking collectives, per_device(): lax.all_to_all(contribution, 'cuts', 0, 0, tiled=True).sum(axis=0)  18.1 us
    ppermute x1, starting transfers between devices, per_device(): lax.ppermute(orbitals[:8], GRID, [((i + 1) % peers, i) for i in range(pee...  12.9 us
    pallas_call x1, Pallas kernels, per_device(): pl.pallas_call(solve_kernel, out_shape=(jax.ShapeDtypeStruct((rows, width...  10.7 us
    pallas_call x1, Pallas kernels, per_device(): pl.pallas_call(functools.partial(gram_kernel, width * groups), out_shape=...  3.25 us
  transfers between devices with their start and end apart: 1, of which 0 were waited for; matrix products, arithmetic and copies ran while one was open for 0% of the time, Pallas kernels for 3%

profile of v3, /device:TPU:1, one launch (start us, length us, event | category | flops | bytes accessed | tf_op | source)
XLA Modules:
  0.0 101.7 jit_solution(1354051555737582253)
XLA Ops:
  0.6 0.7 slice.3
  1.3 12.9 %collective-permute-start = (bf16[8,256]{1,0:T(8,128)(2,1)S(1)}, bf16[8,256]{1,0:T(8,128)(2,1)S(1)}, u32[]{:S(2)}, u32[]{:S(2)}) collective-permute-start(bf16[8,256]{1,0:T(8,128)(2,1)S(1)} %slice.3), channel_id=1, source_target_pairs={{1,0},{2,1},{3,2},{4,3},{5,4},{6,5},{7,6},{8,7},{9,8},{10,9},{11,1... | collective-permute-start | bytes 12296 | tf_op jit(solution)/shard_map/ppermute | solution.py:260
  14.8 0.0 copy-start
  14.8 1.6 %copy-done = bf16[4096,256]{1,0:T(8,128)(2,1)S(1)} copy-done((bf16[4096,256]{1,0:T(8,128)(2,1)S(1)}, bf16[4096,256]{1,0:T(8,128)(2,1)}, u32[]{:S(2)}) %copy-start) | copy-done | bytes 2097176
  16.4 3.3 %gram.1 = (f32[544,128]{1,0:T(8,128)S(1)}, bf16[16,256]{1,0:T(8,128)(2,1)S(1)}, f32[1,256]{1,0:T(1,128)S(1)}) custom-call(bf16[4096,256]{1,0:T(8,128)(2,1)S(1)} %copy-done, f32[32,128]{1,0:T(8,128)} %bitcast.16, s32[1,256]{1,0:T(1,128)} %bitcast.17, s32[1,1]{1,0:T(1,128)} %bitcast.13.count_ref), custom_call_target="tpu_custom_call" | custom-call | tf_op jit(solution)/shard_map/gram/pallas_call | solution.py:262
  19.7 0.0 collective-permute-done.next_ref
  19.7 0.2 border.1
  19.9 26.9 %all_to_all.15.arrived_ref = f32[32,1,2176]{2,1,0:T(1,128)S(1)} all-to-all(f32[32,1,2176]{2,1,0:T(1,128)S(1)} %bitcast.15), channel_id=1, replica_groups=mesh['cuts'=16,'grid_0'=16,'grid_1'=2] {'grid_0','grid_1'}, dimensions={0} | all-to-all | bytes 557056 | tf_op jit(solution)/shard_map/all_to_all | solution.py:276
  46.8 0.0 copy-start.1
  46.8 0.0 copy-start.2
  46.8 0.1 spread.1
  46.9 25.3 %all_to_all.16 = f32[32,1,2176]{2,1,0:T(1,128)S(1)} all-to-all(f32[32,1,2176]{2,1,0:T(1,128)S(1)} %spread.1), channel_id=1, replica_groups=mesh['cuts'=16,'grid_0'=16,'grid_1'=2] {'grid_0','grid_1'}, dimensions={0} | all-to-all | bytes 557056 | tf_op jit(solution)/shard_map/all_to_all | solution.py:278
  72.2 10.7 %solve.1 = (bf16[4096,256]{1,0:T(8,128)(2,1)}, f32[16,32,128]{2,1,0:T(8,128)S(1)}) custom-call(f32[544,128]{1,0:T(8,128)S(1)} %bitcast.14, bf16[4096,256]{1,0:T(8,128)(2,1)} %psi_ref.3, f32[1,256]{1,0:T(1,128)S(1)} %get-tuple-element.9.weights_ref), custom_call_target="tpu_custom_call" | custom-call | tf_op jit(solution)/shard_map/solve/pallas_call | solution.py:279
  83.0 18.1 %all_to_all.17 = f32[16,32,128]{2,1,0:T(8,128)S(1)} all-to-all(f32[16,32,128]{2,1,0:T(8,128)S(1)} %get-tuple-element.11), channel_id=1, replica_groups=mesh['cuts'=16,'grid_0'=16,'grid_1'=2] {'cuts'}, dimensions={0} | all-to-all | bytes 524288 | tf_op jit(solution)/shard_map/all_to_all | solution.py:303
  101.1 0.0 copy-done.1
  101.1 0.0 copy-done.2
  101.1 0.6 fusion.2
  (1 shorter events, 0.0 us)
Async XLA Ops:
  1.3 18.4 %collective-permute-start = (bf16[8,256]{1,0:T(8,128)(2,1)S(1)}, bf16[8,256]{1,0:T(8,128)(2,1)S(1)}, u32[]{:S(2)}, u32[]{:S(2)}) collective-permute-start(bf16[8,256]{1,0:T(8,128)(2,1)S(1)} %slice.3), channel_id=1, source_target_pairs={{1,0},{2,1},{3,2},{4,3},{5,4},{6,5},{7,6},{8,7},{9,8},{10,9},{11,1... | collective-permute-start | bytes 12296 | tf_op jit(solution)/shard_map/ppermute | solution.py:260
  14.8 1.6 %copy-start = (bf16[4096,256]{1,0:T(8,128)(2,1)S(1)}, bf16[4096,256]{1,0:T(8,128)(2,1)}, u32[]{:S(2)}) copy-start(bf16[4096,256]{1,0:T(8,128)(2,1)} %psi_ref.3) | copy-start | bytes 6291460
  46.8 54.2 %copy-start.1 = (f32[4096]{0:T(1024)S(1)}, f32[4096]{0:T(1024)}, u32[]{:S(2)}) copy-start(f32[4096]{0:T(1024)} %param.6) | copy-start | bytes 49156
  46.8 54.3 %copy-start.2 = (f32[4096]{0:T(1024)S(1)}, f32[4096]{0:T(1024)}, u32[]{:S(2)}) copy-start(f32[4096]{0:T(1024)} %param.7) | copy-start | bytes 49156

commit v4 on v3

--- a/solution.py
+++ b/solution.py
@@ -8,7 +8,8 @@
 from jax.sharding import Mesh
 from jax.sharding import PartitionSpec as P
 
-GRID = ("grid_0", "grid_1")
+GRID = ("z_hi", "z_lo", "x_lo")
+EXCHANGE = ('z_lo', 'z_hi', 'x_lo')
 HIGHEST = lax.Precision.HIGHEST
 F32 = jnp.float32
 BF16 = jnp.bfloat16
@@ -273,9 +274,9 @@
     packed = pl.pallas_call(border_kernel, out_shape=pltpu.VMEM((17 * width // 8, 128), F32), name="border")(
         in_vmem(packed), in_vmem(last), in_vmem(following)
     )
-    mine = lax.all_to_all(packed.reshape(peers, 1, chunk), GRID, 0, 0, tiled=True)
+    mine = lax.all_to_all(packed.reshape(peers, 1, chunk), EXCHANGE, 0, 0, tiled=True)
     copies = pl.pallas_call(functools.partial(spread_kernel, rows * peers), out_shape=pltpu.VMEM((peers, 1, chunk), F32), name="spread")(in_vmem(mine))
-    every = lax.all_to_all(copies, GRID, 0, 0, tiled=True)
+    every = lax.all_to_all(copies, EXCHANGE, 0, 0, tiled=True)
     orbitals_out, contribution = pl.pallas_call(
         solve_kernel,
         out_shape=(
@@ -306,7 +307,7 @@
 
 
 def solution(mesh):
-    torus = Mesh(mesh.devices.reshape(mesh.shape["cuts"], 16, 2), ("cuts", "grid_0", "grid_1"))
+    torus = Mesh(mesh.devices.reshape(mesh.shape["cuts"], 4, 4, 2), ("cuts", "z_hi", "z_lo", "x_lo"))
     in_specs = (P(GRID, "cuts"), P(GRID), P(GRID), P("cuts"), P("cuts"))
     out_specs = (P(GRID, "cuts"), P(GRID))
     return jax.shard_map(

time: 102 us -> 101 us (level); the launches traced: 102 us -> 99.6 us
  blocking collectives: 70.3 us -> 68.1 us
    all_to_all x2, blocking collectives: 52.2 us -> 47.6 us  [the longest x1 25.3 us: per_device(): every = lax.all_to_all(copies, EXCHANGE, 0, 0, tiled=True)]
    all_to_all x1, blocking collectives: 18.1 us -> 20.5 us  [per_device(): lax.all_to_all(contribution, 'cuts', 0, 0, tiled=True).sum(axis=0)]
where the time goes in v4:
time: 101 us; the launch traced here: 99.6 us
  blocking collectives  68.1 us (67%)
  Pallas kernels  14.3 us (14%)
  starting transfers between devices  12.9 us (13%)
  local copies, waits for them, and re-layouts  2.28 us (2%)
  between operations  1.34 us (1%)
    all_to_all x1, blocking collectives, per_device(): every = lax.all_to_all(copies, EXCHANGE, 0, 0, tiled=True)  25.3 us
    all_to_all x1, blocking collectives, per_device(): lax.all_to_all(packed.reshape(peers, 1, chunk), EXCHANGE, 0, 0, tiled=True)  22.4 us
    all_to_all x1, blocking collectives, per_device(): lax.all_to_all(contribution, 'cuts', 0, 0, tiled=True).sum(axis=0)  20.5 us
    ppermute x1, starting transfers between devices, per_device(): lax.ppermute(orbitals[:8], GRID, [((i + 1) % peers, i) for i in range(pee...  12.9 us
    pallas_call x1, Pallas kernels, per_device(): pl.pallas_call(solve_kernel, out_shape=(jax.ShapeDtypeStruct((rows, width...  10.7 us
    pallas_call x1, Pallas kernels, per_device(): pl.pallas_call(functools.partial(gram_kernel, width * groups), out_shape=...  3.25 us
  transfers between devices with their start and end apart: 1, of which 0 were waited for; matrix products, arithmetic and copies ran while one was open for 0% of the time, Pallas kernels for 3%

profile of v4, /device:TPU:1, one launch (start us, length us, event | category | flops | bytes accessed | tf_op | source)
XLA Modules:
  0.0 99.6 jit_solution(14841641211278088373)
XLA Ops:
  0.6 0.7 slice.3
  1.3 12.9 %collective-permute-start = (bf16[8,256]{1,0:T(8,128)(2,1)S(1)}, bf16[8,256]{1,0:T(8,128)(2,1)S(1)}, u32[]{:S(2)}, u32[]{:S(2)}) collective-permute-start(bf16[8,256]{1,0:T(8,128)(2,1)S(1)} %slice.3), channel_id=1, source_target_pairs={{1,0},{2,1},{3,2},{4,3},{5,4},{6,5},{7,6},{8,7},{9,8},{10,9},{11,1... | collective-permute-start | bytes 12296 | tf_op jit(solution)/shard_map/ppermute | solution.py:261
  14.8 0.0 copy-start
  14.8 1.6 %copy-done = bf16[4096,256]{1,0:T(8,128)(2,1)S(1)} copy-done((bf16[4096,256]{1,0:T(8,128)(2,1)S(1)}, bf16[4096,256]{1,0:T(8,128)(2,1)}, u32[]{:S(2)}) %copy-start) | copy-done | bytes 2097176
  16.4 3.3 %gram.1 = (f32[544,128]{1,0:T(8,128)S(1)}, bf16[16,256]{1,0:T(8,128)(2,1)S(1)}, f32[1,256]{1,0:T(1,128)S(1)}) custom-call(bf16[4096,256]{1,0:T(8,128)(2,1)S(1)} %copy-done, f32[32,128]{1,0:T(8,128)} %bitcast.16, s32[1,256]{1,0:T(1,128)} %bitcast.17, s32[1,1]{1,0:T(1,128)} %bitcast.13.count_ref), custom_call_target="tpu_custom_call" | custom-call | tf_op jit(solution)/shard_map/gram/pallas_call | solution.py:263
  19.7 0.0 collective-permute-done.next_ref
  19.7 0.2 border.1
  19.9 22.4 %all_to_all.15.arrived_ref = f32[32,1,2176]{2,1,0:T(1,128)S(1)} all-to-all(f32[32,1,2176]{2,1,0:T(1,128)S(1)} %bitcast.15), channel_id=1, replica_groups=mesh['cuts'=16,'z_hi'=4,'z_lo'=4,'x_lo'=2] {'z_lo','z_hi','x_lo'}, dimensions={0} | all-to-all | bytes 557056 | tf_op jit(solution)/shard_map/all_to_all | solution.py:277
  42.3 0.0 copy-start.1
  42.3 0.0 copy-start.2
  42.3 0.1 spread.1
  42.4 25.3 %all_to_all.16 = f32[32,1,2176]{2,1,0:T(1,128)S(1)} all-to-all(f32[32,1,2176]{2,1,0:T(1,128)S(1)} %spread.1), channel_id=1, replica_groups=mesh['cuts'=16,'z_hi'=4,'z_lo'=4,'x_lo'=2] {'z_lo','z_hi','x_lo'}, dimensions={0} | all-to-all | bytes 557056 | tf_op jit(solution)/shard_map/all_to_all | solution.py:279
  67.7 10.7 %solve.1 = (bf16[4096,256]{1,0:T(8,128)(2,1)}, f32[16,32,128]{2,1,0:T(8,128)S(1)}) custom-call(f32[544,128]{1,0:T(8,128)S(1)} %bitcast.14, bf16[4096,256]{1,0:T(8,128)(2,1)} %psi_ref.3, f32[1,256]{1,0:T(1,128)S(1)} %get-tuple-element.9.weights_ref), custom_call_target="tpu_custom_call" | custom-call | tf_op jit(solution)/shard_map/solve/pallas_call | solution.py:280
  78.4 20.5 %all_to_all.17 = f32[16,32,128]{2,1,0:T(8,128)S(1)} all-to-all(f32[16,32,128]{2,1,0:T(8,128)S(1)} %get-tuple-element.11), channel_id=1, replica_groups=mesh['cuts'=16,'z_hi'=4,'z_lo'=4,'x_lo'=2] {'cuts'}, dimensions={0} | all-to-all | bytes 524288 | tf_op jit(solution)/shard_map/all_to_all | solution.py:304
  98.9 0.0 copy-done.1
  98.9 0.0 copy-done.2
  98.9 0.6 fusion.2
  (1 shorter events, 0.0 us)
Async XLA Ops:
  1.3 18.4 %collective-permute-start = (bf16[8,256]{1,0:T(8,128)(2,1)S(1)}, bf16[8,256]{1,0:T(8,128)(2,1)S(1)}, u32[]{:S(2)}, u32[]{:S(2)}) collective-permute-start(bf16[8,256]{1,0:T(8,128)(2,1)S(1)} %slice.3), channel_id=1, source_target_pairs={{1,0},{2,1},{3,2},{4,3},{5,4},{6,5},{7,6},{8,7},{9,8},{10,9},{11,1... | collective-permute-start | bytes 12296 | tf_op jit(solution)/shard_map/ppermute | solution.py:261
  14.8 1.6 %copy-start = (bf16[4096,256]{1,0:T(8,128)(2,1)S(1)}, bf16[4096,256]{1,0:T(8,128)(2,1)}, u32[]{:S(2)}) copy-start(bf16[4096,256]{1,0:T(8,128)(2,1)} %psi_ref.3) | copy-start | bytes 6291460
  42.3 56.6 %copy-start.1 = (f32[4096]{0:T(1024)S(1)}, f32[4096]{0:T(1024)}, u32[]{:S(2)}) copy-start(f32[4096]{0:T(1024)} %param.6) | copy-start | bytes 49156
  42.3 56.6 %copy-start.2 = (f32[4096]{0:T(1024)S(1)}, f32[4096]{0:T(1024)}, u32[]{:S(2)}) copy-start(f32[4096]{0:T(1024)} %param.7) | copy-start | bytes 49156
